TPU v7x, 256 devices: a whole 4x4x8 slice. The times are simulated.
256 devices in a mesh: energy: 32 (over x_hi, z, core), seg: 8 (over x_lo, y).
Axes of the slice: x: 4 (x_hi: 2, x_lo: 2; x = x_hi * 2 + x_lo), y: 4, z: 8, core: 2. Of those that a mesh axis runs over, the one named last changes fastest.
Arguments:
- onsite: float32 [8, 384, 384], P('seg'), may hold values from -3 to 8
- coupling: float32 [8, 384, 384], P('seg'), may hold values from -2 to 2
- phonon: float32 [8, 384, 384], P('seg'), may hold values from -1 to 1
- levels: float32 [32], P('energy'), may hold values from 0.5 to 2
- offsets: int32 [2], replicated, may hold values from 1 to 15
Outputs:
- green_fn: float32 [32, 8, 384, 384], P('energy', 'seg')
- self_energy: float32 [32, 8, 384, 384], P('energy', 'seg')
All inputs are finite; a program needn't handle non-finite values.
Results may differ from a plain program's by a relative error of at most 0.0001.
Values sent between devices are 32-bit elements; how exact they have to be, the bound alone decides.
A program may use at most 64 MiB of HBM per device.

v0:
```python
import functools, jax, jax.numpy as jnp
from jax import lax
from jax.experimental import pallas as pl
from jax.experimental.pallas import tpu as pltpu
NB=384
f32=jnp.float32; bf16=jnp.bfloat16

def split(x):
    hi = x.astype(bf16)
    lo = (x - hi.astype(f32)).astype(bf16)
    return hi, lo

def put(ref, x):
    hi, lo = split(x)
    ref[0] = hi
    ref[1] = lo

def put_at(ref, i, x):
    hi, lo = split(x)
    ref[i, 0] = hi
    ref[i, 1] = lo

def dot(a, b):
    return lax.dot_general(a, b, (((1,), (0,)), ((), ())), preferred_element_type=f32)

def dott(a, b):
    return lax.dot_general(a, b, (((1,), (1,)), ((), ())), preferred_element_type=f32)

def mm(a, b, d=dot):
    ah, al = a; bh, bl = b
    return d(ah, bh) + (d(ah, bl) + d(al, bh))

def rd(ref):
    return ref[0], ref[1]
def rd_at(ref, i):
    return ref[i, 0], ref[i, 1]

def chain_kernel(sref, lev_ref, m_ref, c_ref, o_ref, L, P, Q, C, e_s, r_s, b_s, g_s):
    seg = sref[0]
    row = lax.broadcasted_iota(jnp.int32, (NB, NB), 0)
    col = lax.broadcasted_iota(jnp.int32, (NB, NB), 1)
    eye = (row == col).astype(f32)
    lev = lev_ref[0]

    def inv_into(x, s):
        diag = x * eye
        d_row = 1.0 / jnp.sum(diag, axis=0, keepdims=True)
        d_col = 1.0 / jnp.sum(diag, axis=1, keepdims=True)
        e = eye - x * d_row
        put(e_s, e)
        b = eye + e
        r = mm(rd(e_s), rd(e_s))
        put(r_s.at[0], r)
        put(b_s, b)
        b = b + mm(rd(r_s.at[0]), rd(b_s))
        r = mm(rd(r_s.at[0]), rd(r_s.at[0]))
        put(r_s.at[1], r)
        put(b_s, b)
        b = b + mm(rd(r_s.at[1]), rd(b_s))
        r = mm(rd(r_s.at[1]), rd(r_s.at[1]))
        put(r_s.at[0], r)
        put(b_s, b)
        b = b + mm(rd(r_s.at[0]), rd(b_s))
        L[s] = b * d_col

    put_at(C, 0, c_ref[0])
    x0 = m_ref[0] + lev * eye - 0.25 * mm(rd_at(C, 0), rd_at(C, 0), dott)
    inv_into(x0, 0)

    def fwd(s, _):
        put_at(C, s, c_ref[s])
        put(b_s, L[s - 1])
        c = rd_at(C, s)
        q = mm(c, rd(b_s))
        put_at(Q, s, q)
        x = m_ref[s] + lev * eye - mm(rd_at(Q, s), c, dott)
        p = mm(rd(b_s), c, dott)
        put_at(P, s, p)
        inv_into(x, s)
        return 0
    lax.fori_loop(1, 8, fwd, 0)

    o_ref[...] = L[7]
    def bwd(k, _):
        t = 6 - k
        put(g_s, o_ref[...])
        pg = mm(rd_at(P, t + 1), rd(g_s))
        put(e_s, pg)
        o_ref[...] = L[t] + mm(rd(e_s), rd_at(Q, t + 1))
        return 0
    lax.fori_loop(0, 7 - seg, bwd, 0)

def chain(seg, lev, m, c):
    nst = m.shape[0]
    vm = pl.BlockSpec(memory_space=pltpu.VMEM)
    sm = pl.BlockSpec(memory_space=pltpu.SMEM)
    return pl.pallas_call(
        chain_kernel, out_shape=jax.ShapeDtypeStruct((NB, NB), f32),
        in_specs=[sm, sm, vm, vm], out_specs=vm,
        scratch_shapes=[pltpu.VMEM((8, NB, NB), f32), pltpu.VMEM((8, 2, NB, NB), bf16), pltpu.VMEM((8, 2, NB, NB), bf16),
                        pltpu.VMEM((8, 2, NB, NB), bf16),
                        pltpu.VMEM((2, NB, NB), bf16), pltpu.VMEM((2, 2, NB, NB), bf16), pltpu.VMEM((2, NB, NB), bf16),
                        pltpu.VMEM((2, NB, NB), bf16)],
        compiler_params=pltpu.CompilerParams(vmem_limit_bytes=60 << 20),
        name="chain",
    )(seg, lev, m, c)


def gathered(block, axis):
    return lax.all_gather(block, axis, axis=0, tiled=False)


def phonon_kernel(phi_ref, comb_ref, o_ref):
    phi = split(phi_ref[...])
    half = mm(phi, split(comb_ref[...]))
    o_ref[...] = mm(split(half), phi, dott)


def phonon_product(phi, comb):
    vm = pl.BlockSpec(memory_space=pltpu.VMEM)
    return pl.pallas_call(
        phonon_kernel, out_shape=jax.ShapeDtypeStruct((NB, NB), f32),
        in_specs=[vm, vm], out_specs=vm, name="phonon_product",
        compiler_params=pltpu.CompilerParams(vmem_limit_bytes=60 << 20),
    )(phi, comb)


def energy_sum(green, offsets):
    count = lax.axis_size("energy")
    rows = NB // count
    pieces = lax.all_to_all(green.reshape(count, rows, NB), "energy", 0, 0, tiled=True)
    reach = count // 2
    padded = jnp.pad(pieces, ((reach, reach), (0, 0), (0, 0)))

    def moved(amount):
        return lax.dynamic_slice_in_dim(padded, reach - amount, count, 0)

    combined = moved(offsets[0]) + moved(offsets[1]) + moved(-offsets[0]) + moved(-offsets[1])
    return lax.all_to_all(combined, "energy", 0, 0, tiled=True).reshape(NB, NB)


def shards(onsite, coupling, phonon, levels, offsets):
    seg = lax.axis_index("seg").astype(jnp.int32).reshape(1)
    onsite_all = gathered(onsite[0], "seg")
    coupling_all = gathered(coupling[0], "seg")
    green = chain(seg, levels, onsite_all, coupling_all)
    self_energy = phonon_product(phonon[0], energy_sum(green, offsets))
    green = chain(seg, levels, onsite_all + gathered(self_energy, "seg"), coupling_all)
    return green[None, None], self_energy[None, None]


def solution(mesh):
    P = jax.sharding.PartitionSpec
    in_specs = (P("seg", None, None), P("seg", None, None), P("seg", None, None), P("energy"), P())
    out_specs = (P("energy", "seg", None, None), P("energy", "seg", None, None))
    return jax.shard_map(shards, mesh=mesh, in_specs=in_specs, out_specs=out_specs, check_vma=False)
```

profile of v0, /device:TPU:1, one launch (start us, length us, event | category | flops | bytes accessed | tf_op | source)
XLA Modules:
  0.0 390.2 jit_solution(538105133002571520)
XLA Ops:
  7.2 0.0 all-gather.5.cloned.1.call-start
  7.2 0.7 all-gather.5.cloned.1.call-update
  7.9 0.0 all-gather.7.cloned.1.call-start
  7.9 0.7 all-gather.7.cloned.1.call-update
  9.3 64.1 %all-gather.5.cloned.1.call-done.m_ref = f32[8,384,384]{2,1,0:T(8,128)} async-done(((f32[1,384,384]{2,1,0:T(8,128)}), f32[8,384,384]{2,1,0:T(8,128)}) %all-gather.5.cloned.1.call-update) | async-done | bytes 4718608 | tf_op jit(solution)/shard_map/all_gather | solution.py:110
  73.4 60.6 %all-gather.7.cloned.1.call-done.c_ref = f32[8,384,384]{2,1,0:T(8,128)} async-done(((f32[1,384,384]{2,1,0:T(8,128)}), f32[8,384,384]{2,1,0:T(8,128)}) %all-gather.7.cloned.1.call-update) | async-done | bytes 4718608 | tf_op jit(solution)/shard_map/all_gather | solution.py:110
  134.0 0.0 copy-start
  134.0 60.4 %chain.2 = f32[384,384]{1,0:T(8,128)} custom-call(s32[1]{0:T(128)} %bitcast.sref, f32[1]{0:T(128)S(6)} %copy.7.lev_ref, f32[8,384,384]{2,1,0:T(8,128)} %all-gather.5.cloned.1.call-done.m_ref, f32[8,384,384]{2,1,0:T(8,128)} %all-gather.7.cloned.1.call-done.c_ref), custom_call_target="tpu_custom_call" | custom-call | tf_op jit(solution)/shard_map/chain/pallas_call | solution.py:97
  194.4 2.0 reshape.32
  196.4 10.1 %all-to-all-start = ((f32[32,12,384]{2,1,0:T(8,128)}), f32[32,12,384]{2,1,0:T(8,128)S(1)}, u32[]{:S(2)}, u32[]{:S(2)}) async-start(f32[32,12,384]{2,1,0:T(8,128)} %reshape.32), calls=%async_computation | async-start | bytes 1572864 | tf_op jit(solution)/shard_map/all_to_all | solution.py:131
  206.6 0.2 all-gather.9.cloned.1.call-start
  206.8 0.0 copy-done
  206.8 0.6 fusion.3
  211.3 18.1 %all-to-all-done = f32[32,12,384]{2,1,0:T(8,128)S(1)} async-done(((f32[32,12,384]{2,1,0:T(8,128)}), f32[32,12,384]{2,1,0:T(8,128)S(1)}, u32[]{:S(2)}, u32[]{:S(2)}) %all-to-all-start) | async-done | bytes 589856 | tf_op jit(solution)/shard_map/all_to_all | solution.py:131
  229.3 0.6 fusion.2
  230.0 28.1 %all_to_all.10 = f32[32,12,384]{2,1,0:T(8,128)S(1)} all-to-all(f32[32,12,384]{2,1,0:T(8,128)S(1)} %fusion.2), channel_id=1, replica_groups=mesh['energy'=32,'seg'=8] {'energy'}, dimensions={0} | all-to-all | bytes 1179648 | tf_op jit(solution)/shard_map/all_to_all | solution.py:139
  258.1 0.9 reshape.33.comb_ref
  259.0 3.6 phonon_product.1
  262.6 0.0 all-gather.9.cloned.1.call-update
  262.7 54.1 %all-gather.9.cloned.1.call-done = f32[3072,384]{1,0:T(8,128)} async-done(((f32[384,384]{1,0:T(8,128)}), f32[3072,384]{1,0:T(8,128)}) %all-gather.9.cloned.1.call-update) | async-done | bytes 4718608 | tf_op jit(solution)/shard_map/all_gather | solution.py:110
  316.8 6.5 %add.49.m_ref = f32[8,384,384]{2,1,0:T(8,128)} add(f32[8,384,384]{2,1,0:T(8,128)} %all-gather.5.cloned.1.call-done.m_ref, f32[8,384,384]{2,1,0:T(8,128)} %bitcast.13) | non-fusion elementwise | flops 1179648 | bytes 14155776 | tf_op jit(solution)/shard_map/add | solution.py:148
  323.2 60.4 %chain.3 = f32[384,384]{1,0:T(8,128)} custom-call(s32[1]{0:T(128)} %bitcast.sref, f32[1]{0:T(128)S(6)} %copy.7.lev_ref, f32[8,384,384]{2,1,0:T(8,128)} %add.49.m_ref, f32[8,384,384]{2,1,0:T(8,128)} %all-gather.7.cloned.1.call-done.c_ref), custom_call_target="tpu_custom_call" | custom-call | tf_op jit(solution)/shard_map/chain/pallas_call | solution.py:97
Async XLA Ops:
  7.2 66.3 %all-gather.5.cloned.1.call-start = ((), (), s32[]{:S(2)}) async-start(), calls=%async_computation.2 | async-start | bytes 5308416 | tf_op jit(solution)/shard_map/all_gather | solution.py:110
  7.9 126.1 %all-gather.7.cloned.1.call-start = ((), (), s32[]{:S(2)}) async-start(), calls=%async_computation.3 | async-start | bytes 5308416 | tf_op jit(solution)/shard_map/all_gather | solution.py:110
  134.0 72.8 %copy-start = (s32[2]{0:T(128)S(1)}, s32[2]{0:T(128)}, u32[]{:S(2)}) copy-start(s32[2]{0:T(128)} %param.9) | copy-start | bytes 28
  196.4 32.9 %all-to-all-start = ((f32[32,12,384]{2,1,0:T(8,128)}), f32[32,12,384]{2,1,0:T(8,128)S(1)}, u32[]{:S(2)}, u32[]{:S(2)}) async-start(f32[32,12,384]{2,1,0:T(8,128)} %reshape.32), calls=%async_computation | async-start | bytes 1572864 | tf_op jit(solution)/shard_map/all_to_all | solution.py:131
  206.6 110.2 %all-gather.9.cloned.1.call-start = ((), (), s32[]{:S(2)}) async-start(), calls=%async_computation.4 | async-start | bytes 5308416 | tf_op jit(solution)/shard_map/all_gather | solution.py:110
Sparse Core Ops, SparseCore 0:
  9.8 63.6 all-gather.4
  75.2 58.7 all-gather.6
  262.8 53.9 all-gather.8
where the time goes:
time: 390 us
  waiting for transfers between devices  198 us (51%)
  Pallas kernels  124 us (32%)
  blocking collectives  28.1 us (7%)
  between operations  18.3 us (5%)
  starting transfers between devices  10.4 us (3%)
  other arithmetic  7.12 us (2%)
    all_gather x3, waiting for transfers between devices, gathered(): return lax.all_gather(block, axis, axis=0, tiled=False)  179 us
    pallas_call x2, Pallas kernels, chain(): pl.pallas_call(chain_kernel, out_shape=jax.ShapeDtypeStruct((NB, NB), f32...  121 us
    all_to_all x1, blocking collectives, energy_sum(): return lax.all_to_all(combined, 'energy', 0, 0, tiled=True).reshape(NB, NB)  28.1 us
    all_to_all x1, waiting for transfers between devices, energy_sum(): lax.all_to_all(green.reshape(count, rows, NB), 'energy', 0, 0, tiled=True)  18.1 us
    all_to_all x1, starting transfers between devices, energy_sum(): lax.all_to_all(green.reshape(count, rows, NB), 'energy', 0, 0, tiled=True)  10.1 us
  transfers between devices with their start and end apart: 4, of which 4 were waited for; matrix products, arithmetic and copies ran while one was open for 0% of the time, Pallas kernels for 0%

commit v1 on v0

v1 whole, which is shorter than its diff:
```python
import functools
import jax
import jax.numpy as jnp
from jax import lax
from jax.experimental import pallas as pl
from jax.experimental.pallas import tpu as pltpu

NB = 384
SEGS = 8
f32 = jnp.float32
bf16 = jnp.bfloat16
MESH = pl.DeviceIdType.MESH


def split(x):
    hi = x.astype(bf16)
    lo = (x - hi.astype(f32)).astype(bf16)
    return hi, lo


def put(ref, x):
    hi, lo = split(x)
    ref[0] = hi
    ref[1] = lo


def rd(ref):
    return ref[0], ref[1]


def dot(a, b):
    return lax.dot_general(a, b, (((1,), (0,)), ((), ())), preferred_element_type=f32)


def dott(a, b):
    return lax.dot_general(a, b, (((1,), (1,)), ((), ())), preferred_element_type=f32)


def mm(a, b, d=dot):
    ah, al = a
    bh, bl = b
    return d(ah, bh) + (d(ah, bl) + d(al, bh))


def table(seg, values):
    out = jnp.int32(values[-1])
    for i, v in enumerate(values[:-1]):
        out = jnp.where(seg == i, jnp.int32(v), out)
    return out


class Gather:
    def __init__(self, bufs, rsem, psem, ssem, dsem, dssem, halves):
        self.bufs, self.rsem, self.psem, self.ssem, self.dsem, self.dssem = bufs, rsem, psem, ssem, dsem, dssem
        e = lax.axis_index("energy")
        self.seg = lax.axis_index("seg")
        core = e % 2
        self.sibling = {"energy": e + 1 - 2 * core}
        pair, y = self.seg // 4, self.seg % 4
        at = lambda p, dy: p * 4 + (y + dy) % 4
        self.up, self.down, self.two = at(pair, 1), at(pair, 3), at(pair, 2)
        self.cross, self.cup, self.cdown, self.ctwo = at(1 - pair, 0), at(1 - pair, 1), at(1 - pair, 3), at(1 - pair, 2)
        self.halves = halves
        n = NB // 2 if halves else NB
        base = core * n if halves else 0
        self.rows = pl.ds(pl.multiple_of(base, 8), n)
        self.low = pl.ds(pl.multiple_of(base, 8), n // 2)
        self.high = pl.ds(pl.multiple_of(base + n // 2, 8), n // 2)

    def copy(self, a, block, rows, s, sem, to):
        ref = self.bufs[a].at[block, rows]
        return pltpu.make_async_remote_copy(
            src_ref=ref, dst_ref=ref, send_sem=self.ssem.at[a, s], recv_sem=sem,
            device_id=to, device_id_type=MESH)

    def got(self, a, block, rows, sem):
        self.copy(a, block, rows, 0, sem, {"seg": self.up}).wait_recv()

    def send(self, a, i):
        r, p = self.rsem, self.psem
        up, down, cross = {"seg": self.up}, {"seg": self.down}, {"seg": self.cross}
        block, rows, sem, to = (
            (self.seg, self.rows, r.at[a, self.seg], up),
            (self.seg, self.rows, r.at[a, self.seg], down),
            (self.seg, self.rows, r.at[a, self.seg], cross),
            (self.down, self.low, p.at[a, 0], up),
            (self.up, self.high, p.at[a, 1], down),
            (self.cross, self.rows, r.at[a, self.cross], up),
            (self.cross, self.rows, r.at[a, self.cross], down),
            (self.two, self.rows, r.at[a, self.two], cross),
        )[i]
        return self.copy(a, block, rows, i, sem, to)

    def twin(self, a, block):
        ref = self.bufs[a].at[block, self.rows]
        return pltpu.make_async_remote_copy(
            src_ref=ref, dst_ref=ref, send_sem=self.dssem.at[a, block], recv_sem=self.dsem.at[a, block],
            device_id=self.sibling, device_id_type=MESH)

    def pass_on(self, a, block):
        if self.halves:
            self.twin(a, block).start()

    def start(self, a):
        for i in range(3):
            self.send(a, i).start()

    def phase1(self):
        for a in range(len(self.bufs)):
            self.got(a, self.down, self.rows, self.rsem.at[a, self.down])
            self.send(a, 3).start()
            self.got(a, self.up, self.rows, self.rsem.at[a, self.up])
            self.send(a, 4).start()
            self.got(a, self.cross, self.rows, self.rsem.at[a, self.cross])
            self.send(a, 5).start()
            self.send(a, 6).start()
            for b in (self.down, self.up, self.cross):
                self.pass_on(a, b)

    def phase2(self):
        for a in range(len(self.bufs)):
            self.got(a, self.two, self.low, self.psem.at[a, 0])
            self.got(a, self.two, self.high, self.psem.at[a, 1])
            self.send(a, 7).start()
            self.pass_on(a, self.two)

    def phase3(self):
        for a in range(len(self.bufs)):
            for b in (self.cdown, self.cup):
                self.got(a, b, self.rows, self.rsem.at[a, b])
                self.pass_on(a, b)

    def phase4(self):
        for a in range(len(self.bufs)):
            self.got(a, self.ctwo, self.rows, self.rsem.at[a, self.ctwo])
            self.pass_on(a, self.ctwo)

    def phases(self, k):
        seg = self.seg
        for phase, times in ((self.phase1, (1, 0, 0, 0, 0, 0, 0, 0)), (self.phase2, (2, 3, 0, 1, 1, 0, 0, 0)),
                             (self.phase3, (5, 4, 4, 4, 1, 0, 0, 0)), (self.phase4, (6, 7, 4, 5, 2, 3, 0, 1))):
            pl.when(table(seg, times) == k)(phase)

    def need(self, a, k):
        if self.halves:
            @pl.when(k != self.seg)
            def _():
                n = NB // 2
                e = lax.axis_index("energy")
                other = pl.ds(pl.multiple_of((1 - e % 2) * n, 8), n)
                self.got(a, k, other, self.dsem.at[a, k])

    def finish(self):
        for a in range(len(self.bufs)):
            for i in range(8):
                self.send(a, i).wait_send()
            if self.halves:
                for b in (self.down, self.up, self.cross, self.two, self.cdown, self.cup, self.ctwo):
                    self.twin(a, b).wait_send()


def entry_barrier(with_sibling):
    e = lax.axis_index("energy")
    seg = lax.axis_index("seg")
    pair, y = seg // 4, seg % 4
    to = [{"seg": pair * 4 + (y + 1) % 4}, {"seg": pair * 4 + (y + 3) % 4}, {"seg": (1 - pair) * 4 + y}]
    if with_sibling:
        to.append({"energy": e + 1 - 2 * (e % 2)})
    barrier = pltpu.get_barrier_semaphore()
    for d in to:
        pl.semaphore_signal(barrier, inc=1, device_id=d, device_id_type=MESH)
    pl.semaphore_wait(barrier, len(to))


def identity():
    row = lax.broadcasted_iota(jnp.int32, (NB, NB), 0)
    col = lax.broadcasted_iota(jnp.int32, (NB, NB), 1)
    return (row == col).astype(f32)


def invert_into(L, s, x, e_s, r_s, b_s):
    eye = identity()
    diag = x * eye
    d_row = 1.0 / jnp.sum(diag, axis=0, keepdims=True)
    d_col = 1.0 / jnp.sum(diag, axis=1, keepdims=True)
    e = eye - x * d_row
    put(e_s, e)
    b = eye + e
    r = mm(rd(e_s), rd(e_s))
    put(r_s.at[0], r)
    put(b_s, b)
    b = b + mm(rd(r_s.at[0]), rd(b_s))
    r = mm(rd(r_s.at[0]), rd(r_s.at[0]))
    put(r_s.at[1], r)
    put(b_s, b)
    b = b + mm(rd(r_s.at[1]), rd(b_s))
    r = mm(rd(r_s.at[1]), rd(r_s.at[1]))
    put(r_s.at[0], r)
    put(b_s, b)
    b = b + mm(rd(r_s.at[0]), rd(b_s))
    L[s] = b * d_col


def sweep(g, base_at, prepare, C, L, P, Q, e_s, r_s, b_s, out):
    seg = lax.axis_index("seg")
    g.phases(0)
    prepare(0)
    x0 = base_at(0) - 0.25 * mm(rd(C.at[0]), rd(C.at[0]), dott)
    invert_into(L, 0, x0, e_s, r_s, b_s)

    def forward(k, carry):
        g.phases(k)
        prepare(k)
        c = rd(C.at[k])
        put(b_s, L[k - 1])
        put(Q.at[k], mm(c, rd(b_s)))
        x = base_at(k) - mm(rd(Q.at[k]), c, dott)
        put(P.at[k], mm(rd(b_s), c, dott))
        invert_into(L, k, x, e_s, r_s, b_s)
        return carry

    lax.fori_loop(1, SEGS, forward, 0)
    out[...] = L[SEGS - 1]

    def backward(i, carry):
        t = SEGS - 1 - i
        put(b_s, out[...])
        put(e_s, mm(rd(P.at[t]), rd(b_s)))
        out[...] = L[t - 1] + mm(rd(e_s), rd(Q.at[t]))
        return carry

    lax.fori_loop(0, SEGS - 1 - seg, backward, 0)


def first_kernel(lev_ref, m_ref, c_ref, o_ref, call_ref, mall_ref,
                 cb, mb, C, L, P, Q, e_s, r_s, b_s, rsem, psem, ssem, dsem, dssem, lsem):
    seg = lax.axis_index("seg")
    own = [pltpu.make_async_copy(c_ref.at[0], cb.at[seg], lsem.at[0]),
           pltpu.make_async_copy(m_ref.at[0], mb.at[seg], lsem.at[1])]
    for c in own:
        c.start()
    entry_barrier(True)
    g = Gather((cb, mb), rsem, psem, ssem, dsem, dssem, True)
    for a, c in enumerate(own):
        c.wait()
        g.start(a)

    def prepare(k):
        g.need(0, k)
        g.need(1, k)
        put(C.at[k], cb[k])

    def base_at(k):
        return mb[k] + lev_ref[0] * identity()

    sweep(g, base_at, prepare, C, L, P, Q, e_s, r_s, b_s, o_ref)
    out = [pltpu.make_async_copy(cb, call_ref, lsem.at[0]), pltpu.make_async_copy(mb, mall_ref, lsem.at[1])]
    for c in out:
        c.start()
    g.finish()
    for c in out:
        c.wait()


def second_kernel(lev_ref, phi_ref, comb_ref, m_ref, c_ref, o_ref, se_ref,
                  sb, mb, cb, C, L, P, Q, e_s, r_s, b_s, rsem, psem, ssem, lsem):
    seg = lax.axis_index("seg")
    local = [pltpu.make_async_copy(c_ref, cb, lsem.at[0]), pltpu.make_async_copy(m_ref, mb, lsem.at[1])]
    for c in local:
        c.start()
    phi = split(phi_ref[0])
    half = mm(phi, split(comb_ref[...]))
    sb[seg] = mm(split(half), phi, dott)
    entry_barrier(False)
    g = Gather((sb,), rsem, psem, ssem, None, None, False)
    se_ref[...] = sb[seg]
    g.start(0)
    for c in local:
        c.wait()

    def prepare(k):
        put(C.at[k], cb[k])

    def base_at(k):
        return mb[k] + lev_ref[0] * identity() + sb[k]

    sweep(g, base_at, prepare, C, L, P, Q, e_s, r_s, b_s, o_ref)
    g.finish()


def block(n=None):
    return pltpu.VMEM((NB, NB) if n is None else (n, NB, NB), f32)


def pairs(n=None):
    return pltpu.VMEM((2, NB, NB) if n is None else (n, 2, NB, NB), bf16)


WORK = [pairs(8), block(8), pairs(8), pairs(8), pairs(), pairs(2), pairs()]
DMA = pltpu.SemaphoreType.DMA
VM = pl.BlockSpec(memory_space=pltpu.VMEM)
SM = pl.BlockSpec(memory_space=pltpu.SMEM)
ANY = pl.BlockSpec(memory_space=pl.ANY)
ONE = jax.ShapeDtypeStruct((NB, NB), f32)
ALL = jax.ShapeDtypeStruct((SEGS, NB, NB), f32)


def first_round(levels, onsite, coupling):
    return pl.pallas_call(
        first_kernel, out_shape=(ONE, ALL, ALL),
        in_specs=[SM, ANY, ANY], out_specs=(VM, ANY, ANY),
        scratch_shapes=[block(8), block(8)] + WORK + [DMA((2, 8)), DMA((2, 2)), DMA((2, 8)), DMA((2, 8)), DMA((2, 8)), DMA((2,))],
        compiler_params=pltpu.CompilerParams(vmem_limit_bytes=60 << 20, collective_id=0, has_side_effects=True),
        name="first_round",
    )(levels, onsite, coupling)


def second_round(levels, phonon, combined, onsite_all, coupling_all):
    return pl.pallas_call(
        second_kernel, out_shape=(ONE, ONE),
        in_specs=[SM, VM, VM, ANY, ANY], out_specs=(VM, VM),
        scratch_shapes=[block(8), block(8), block(8)] + WORK + [DMA((1, 8)), DMA((1, 2)), DMA((1, 8)), DMA((2,))],
        compiler_params=pltpu.CompilerParams(vmem_limit_bytes=60 << 20, collective_id=1, has_side_effects=True),
        name="second_round",
    )(levels, phonon, combined, onsite_all, coupling_all)


def energy_sum(green, offsets):
    count = lax.axis_size("energy")
    rows = NB // count
    pieces = lax.all_to_all(green.reshape(count, rows, NB), "energy", 0, 0, tiled=True)
    reach = count // 2
    padded = jnp.pad(pieces, ((reach, reach), (0, 0), (0, 0)))

    def moved(amount):
        return lax.dynamic_slice_in_dim(padded, reach - amount, count, 0)

    combined = moved(offsets[0]) + moved(offsets[1]) + moved(-offsets[0]) + moved(-offsets[1])
    return lax.all_to_all(combined, "energy", 0, 0, tiled=True).reshape(NB, NB)


def shards(onsite, coupling, phonon, levels, offsets):
    green, coupling_all, onsite_all = first_round(levels, onsite, coupling)
    combined = energy_sum(green, offsets)
    green, self_energy = second_round(levels, phonon, combined, onsite_all, coupling_all)
    return green[None, None], self_energy[None, None]


def solution(mesh):
    spec = jax.sharding.PartitionSpec
    block_in = spec("seg", None, None)
    block_out = spec("energy", "seg", None, None)
    return jax.shard_map(shards, mesh=mesh, in_specs=(block_in, block_in, block_in, spec("energy"), spec()),
                         out_specs=(block_out, block_out), check_vma=False)
```

time: 390 us -> 252 us (0.65)
  the two profiles are of different devices: /device:TPU:1 before, /device:TPU:15 now
where the time goes in v1:
time: 252 us; the launch traced here: 248 us
  Pallas kernels  177 us (70%)
  blocking collectives  28.1 us (11%)
  waiting for transfers between devices  15.8 us (6%)
  starting transfers between devices  12.7 us (5%)
  local copies, waits for them, and re-layouts  8.03 us (3%)
  between operations  5.21 us (2%)
    pallas_call x1, Pallas kernels, first_round(): pl.pallas_call(first_kernel, out_shape=(ONE, ALL, ALL), in_specs=[SM, ANY...  91.5 us
    pallas_call x1, Pallas kernels, second_round(): pl.pallas_call(second_kernel, out_shape=(ONE, ONE), in_specs=[SM, VM, VM,...  85.9 us
    all_to_all x1, blocking collectives, energy_sum(): return lax.all_to_all(combined, 'energy', 0, 0, tiled=True).reshape(NB, NB)  28.1 us
    all_to_all x1, waiting for transfers between devices, energy_sum(): lax.all_to_all(green.reshape(count, rows, NB), 'energy', 0, 0, tiled=True)  15.8 us
    all_to_all x1, starting transfers between devices, energy_sum(): lax.all_to_all(green.reshape(count, rows, NB), 'energy', 0, 0, tiled=True)  12.7 us
  transfers between devices with their start and end apart: 1, of which 1 were waited for; matrix products, arithmetic and copies ran while one was open for 1% of the time, Pallas kernels for 0%

profile of v1, /device:TPU:15, one launch (start us, length us, event | category | flops | bytes accessed | tf_op | source)
XLA Modules:
  0.0 248.0 jit_solution(16748402779573374495)
XLA Ops:
  1.3 91.5 %first_round.1 = (f32[384,384]{1,0:T(8,128)}, f32[8,384,384]{2,1,0:T(8,128)}, f32[8,384,384]{2,1,0:T(8,128)}) custom-call(f32[1]{0:T(128)S(6)} %copy.9.lev_ref, f32[1,384,384]{2,1,0:T(8,128)} %m_ref.1, f32[1,384,384]{2,1,0:T(8,128)} %c_ref.1), custom_call_target="tpu_custom_call" | custom-call | tf_op jit(solution)/shard_map/first_round/pallas_call | solution.py:309
  92.8 2.0 reshape.28
  94.8 12.7 %all-to-all-start = ((f32[32,12,384]{2,1,0:T(8,128)}), f32[32,12,384]{2,1,0:T(8,128)S(1)}, u32[]{:S(2)}, u32[]{:S(2)}) async-start(f32[32,12,384]{2,1,0:T(8,128)} %reshape.28), calls=%async_computation | async-start | bytes 1572864 | tf_op jit(solution)/shard_map/all_to_all | solution.py:331
  107.5 1.3 fusion.3
  112.7 15.8 %all-to-all-done = f32[32,12,384]{2,1,0:T(8,128)S(1)} async-done(((f32[32,12,384]{2,1,0:T(8,128)}), f32[32,12,384]{2,1,0:T(8,128)S(1)}, u32[]{:S(2)}, u32[]{:S(2)}) %all-to-all-start) | async-done | bytes 589856 | tf_op jit(solution)/shard_map/all_to_all | solution.py:331
  128.6 0.7 fusion.2
  129.2 28.1 %all_to_all.10 = f32[32,12,384]{2,1,0:T(8,128)S(1)} all-to-all(f32[32,12,384]{2,1,0:T(8,128)S(1)} %fusion.2), channel_id=1, replica_groups=mesh['energy'=32,'seg'=8] {'energy'}, dimensions={0} | all-to-all | bytes 1179648 | tf_op jit(solution)/shard_map/all_to_all | solution.py:339
  157.3 0.9 reshape.29.comb_ref
  158.2 85.9 %second_round.1 = (f32[384,384]{1,0:T(8,128)}, f32[384,384]{1,0:T(8,128)}) custom-call(f32[1]{0:T(128)S(6)} %copy.9.lev_ref, f32[1,384,384]{2,1,0:T(8,128)} %phi_ref.1, f32[384,384]{1,0:T(8,128)} %reshape.29.comb_ref, f32[8,384,384]{2,1,0:T(8,128)} %get-tuple-element.8.m_ref, f32[8,384,384]{2,1,0:T(8,128)} %get-tuple-element.9.c_ref), custom_call_target="tpu_custom_call" | custom-call | tf_op jit(solution)/shard_map/second_round/pallas_call | solution.py:319
  244.1 1.9 copy.10
  246.1 1.9 copy.11
Async XLA Ops:
  94.8 33.8 %all-to-all-start = ((f32[32,12,384]{2,1,0:T(8,128)}), f32[32,12,384]{2,1,0:T(8,128)S(1)}, u32[]{:S(2)}, u32[]{:S(2)}) async-start(f32[32,12,384]{2,1,0:T(8,128)} %reshape.28), calls=%async_computation | async-start | bytes 1572864 | tf_op jit(solution)/shard_map/all_to_all | solution.py:331

commit v2 on v1

--- a/solution.py
+++ b/solution.py
@@ -7,6 +7,10 @@
 
 NB = 384
 SEGS = 8
+ENERGIES = 32
+CHIPS = ENERGIES // 2
+SLAB = NB // CHIPS
+PAD = 15
 f32 = jnp.float32
 bf16 = jnp.bfloat16
 MESH = pl.DeviceIdType.MESH
@@ -159,17 +163,26 @@
                     self.twin(a, b).wait_send()
 
 
-def entry_barrier(with_sibling):
+def entry_barrier():
     e = lax.axis_index("energy")
     seg = lax.axis_index("seg")
+    core = e % 2
     pair, y = seg // 4, seg % 4
-    to = [{"seg": pair * 4 + (y + 1) % 4}, {"seg": pair * 4 + (y + 3) % 4}, {"seg": (1 - pair) * 4 + y}]
-    if with_sibling:
-        to.append({"energy": e + 1 - 2 * (e % 2)})
     barrier = pltpu.get_barrier_semaphore()
-    for d in to:
-        pl.semaphore_signal(barrier, inc=1, device_id=d, device_id_type=MESH)
-    pl.semaphore_wait(barrier, len(to))
+
+    def hello(to):
+        pl.semaphore_signal(barrier, inc=1, device_id=to, device_id_type=MESH)
+
+    for other in (pair * 4 + (y + 1) % 4, pair * 4 + (y + 3) % 4, (1 - pair) * 4 + y):
+        hello({"seg": other})
+    for d in range(1, 32):
+        other = (e + d) % 32
+
+        @pl.when((core == 1) | (other % 2 == 1))
+        def _():
+            hello({"energy": other})
+
+    pl.semaphore_wait(barrier, 3 + 16 + 15 * core)
 
 
 def identity():
@@ -232,14 +245,101 @@
     lax.fori_loop(0, SEGS - 1 - seg, backward, 0)
 
 
-def first_kernel(lev_ref, m_ref, c_ref, o_ref, call_ref, mall_ref,
-                 cb, mb, C, L, P, Q, e_s, r_s, b_s, rsem, psem, ssem, dsem, dssem, lsem):
+def exchange(green, off_ref, got, slabs, combined, out_ssem, out_rsem, back_ssem, back_rsem):
+    e = lax.axis_index("energy")
+    core, chip = e % 2, e // 2
+    adder = core == 1
+
+    def slab_rows(j):
+        return pl.ds(pl.multiple_of(j * SLAB, 8), SLAB)
+
+    def out_copy(j, source):
+        return pltpu.make_async_remote_copy(
+            src_ref=green.at[slab_rows(j)], dst_ref=got.at[PAD + source], send_sem=out_ssem.at[j], recv_sem=out_rsem.at[source],
+            device_id={"energy": 2 * j + 1}, device_id_type=MESH)
+
+    def back_copy(energy, j):
+        return pltpu.make_async_remote_copy(
+            src_ref=slabs.at[energy], dst_ref=combined.at[slab_rows(j)], send_sem=back_ssem.at[energy], recv_sem=back_rsem.at[j],
+            device_id={"energy": energy}, device_id_type=MESH)
+
+    def send_out(d, carry):
+        j = (chip + d) % CHIPS
+
+        @pl.when(e != 2 * j + 1)
+        def _():
+            out_copy(j, e).start()
+        return carry
+
+    lax.fori_loop(0, CHIPS, send_out, 0)
+
+    @pl.when(adder)
+    def _():
+        got[PAD + e] = green[slab_rows(chip)]
+        edge = jnp.zeros((SLAB, NB), f32)
+        for i in range(PAD):
+            got[i] = edge
+            got[PAD + ENERGIES + i] = edge
+
+        def receive(d, carry):
+            source = (e + d) % ENERGIES
+            out_copy(chip, source).wait_recv()
+            return carry
+
+        lax.fori_loop(1, ENERGIES, receive, 0)
+        o1, o2 = off_ref[0], off_ref[1]
+
+        def add(i, carry):
+            p = PAD + i
+            slabs[i] = got[p - o1] + got[p - o2] + got[p + o1] + got[p + o2]
+            return carry
+
+        lax.fori_loop(0, ENERGIES, add, 0)
+        combined[slab_rows(chip)] = slabs[e]
+
+        def send_back(d, carry):
+            back_copy((e + d) % ENERGIES, chip).start()
+            return carry
+
+        lax.fori_loop(1, ENERGIES, send_back, 0)
+
+    def receive_back(j, carry):
+        @pl.when(e != 2 * j + 1)
+        def _():
+            back_copy(e, j).wait_recv()
+        return carry
+
+    lax.fori_loop(0, CHIPS, receive_back, 0)
+
+    def finish():
+        def sent_out(j, carry):
+            @pl.when(e != 2 * j + 1)
+            def _():
+                out_copy(j, e).wait_send()
+            return carry
+
+        lax.fori_loop(0, CHIPS, sent_out, 0)
+
+        @pl.when(adder)
+        def _():
+            def sent_back(d, carry):
+                back_copy((e + d) % ENERGIES, chip).wait_send()
+                return carry
+
+            lax.fori_loop(1, ENERGIES, sent_back, 0)
+
+    return finish
+
+
+def whole_kernel(lev_ref, off_ref, phi_ref, m_ref, c_ref, o_ref, se_ref,
+                 cb, mb, sb, C, L, P, Q, e_s, r_s, b_s, green, got, slabs, combined,
+                 rsem, psem, ssem, dsem, dssem, rsem2, psem2, ssem2, out_ssem, out_rsem, back_ssem, back_rsem, lsem):
     seg = lax.axis_index("seg")
     own = [pltpu.make_async_copy(c_ref.at[0], cb.at[seg], lsem.at[0]),
            pltpu.make_async_copy(m_ref.at[0], mb.at[seg], lsem.at[1])]
     for c in own:
         c.start()
-    entry_barrier(True)
+    entry_barrier()
     g = Gather((cb, mb), rsem, psem, ssem, dsem, dssem, True)
     for a, c in enumerate(own):
         c.wait()
@@ -253,39 +353,18 @@
     def base_at(k):
         return mb[k] + lev_ref[0] * identity()
 
-    sweep(g, base_at, prepare, C, L, P, Q, e_s, r_s, b_s, o_ref)
-    out = [pltpu.make_async_copy(cb, call_ref, lsem.at[0]), pltpu.make_async_copy(mb, mall_ref, lsem.at[1])]
-    for c in out:
-        c.start()
+    sweep(g, base_at, prepare, C, L, P, Q, e_s, r_s, b_s, green)
+    finish = exchange(green, off_ref, got, slabs, combined, out_ssem, out_rsem, back_ssem, back_rsem)
+    phi = split(phi_ref[0])
+    half = mm(phi, split(combined[...]))
+    sb[seg] = mm(split(half), phi, dott)
+    g2 = Gather((sb,), rsem2, psem2, ssem2, None, None, False)
+    g2.start(0)
+    se_ref[...] = sb[seg]
+    sweep(g2, lambda k: base_at(k) + sb[k], lambda k: None, C, L, P, Q, e_s, r_s, b_s, o_ref)
+    finish()
     g.finish()
-    for c in out:
-        c.wait()
-
-
-def second_kernel(lev_ref, phi_ref, comb_ref, m_ref, c_ref, o_ref, se_ref,
-                  sb, mb, cb, C, L, P, Q, e_s, r_s, b_s, rsem, psem, ssem, lsem):
-    seg = lax.axis_index("seg")
-    local = [pltpu.make_async_copy(c_ref, cb, lsem.at[0]), pltpu.make_async_copy(m_ref, mb, lsem.at[1])]
-    for c in local:
-        c.start()
-    phi = split(phi_ref[0])
-    half = mm(phi, split(comb_ref[...]))
-    sb[seg] = mm(split(half), phi, dott)
-    entry_barrier(False)
-    g = Gather((sb,), rsem, psem, ssem, None, None, False)
-    se_ref[...] = sb[seg]
-    g.start(0)
-    for c in local:
-        c.wait()
-
-    def prepare(k):
-        put(C.at[k], cb[k])
-
-    def base_at(k):
-        return mb[k] + lev_ref[0] * identity() + sb[k]
-
-    sweep(g, base_at, prepare, C, L, P, Q, e_s, r_s, b_s, o_ref)
-    g.finish()
+    g2.finish()
 
 
 def block(n=None):
@@ -305,44 +384,22 @@
 ALL = jax.ShapeDtypeStruct((SEGS, NB, NB), f32)
 
 
-def first_round(levels, onsite, coupling):
+def whole(levels, offsets, phonon, onsite, coupling):
     return pl.pallas_call(
-        first_kernel, out_shape=(ONE, ALL, ALL),
-        in_specs=[SM, ANY, ANY], out_specs=(VM, ANY, ANY),
-        scratch_shapes=[block(8), block(8)] + WORK + [DMA((2, 8)), DMA((2, 2)), DMA((2, 8)), DMA((2, 8)), DMA((2, 8)), DMA((2,))],
-        compiler_params=pltpu.CompilerParams(vmem_limit_bytes=60 << 20, collective_id=0, has_side_effects=True),
-        name="first_round",
-    )(levels, onsite, coupling)
-
-
-def second_round(levels, phonon, combined, onsite_all, coupling_all):
-    return pl.pallas_call(
-        second_kernel, out_shape=(ONE, ONE),
-        in_specs=[SM, VM, VM, ANY, ANY], out_specs=(VM, VM),
-        scratch_shapes=[block(8), block(8), block(8)] + WORK + [DMA((1, 8)), DMA((1, 2)), DMA((1, 8)), DMA((2,))],
-        compiler_params=pltpu.CompilerParams(vmem_limit_bytes=60 << 20, collective_id=1, has_side_effects=True),
-        name="second_round",
-    )(levels, phonon, combined, onsite_all, coupling_all)
-
-
-def energy_sum(green, offsets):
-    count = lax.axis_size("energy")
-    rows = NB // count
-    pieces = lax.all_to_all(green.reshape(count, rows, NB), "energy", 0, 0, tiled=True)
-    reach = count // 2
-    padded = jnp.pad(pieces, ((reach, reach), (0, 0), (0, 0)))
-
-    def moved(amount):
-        return lax.dynamic_slice_in_dim(padded, reach - amount, count, 0)
-
-    combined = moved(offsets[0]) + moved(offsets[1]) + moved(-offsets[0]) + moved(-offsets[1])
-    return lax.all_to_all(combined, "energy", 0, 0, tiled=True).reshape(NB, NB)
+        whole_kernel, out_shape=(ONE, ONE),
+        in_specs=[SM, SM, VM, ANY, ANY], out_specs=(VM, VM),
+        scratch_shapes=[block(8), block(8), block(8)] + WORK + [
+            block(), pltpu.VMEM((ENERGIES + 2 * PAD, SLAB, NB), f32), pltpu.VMEM((ENERGIES, SLAB, NB), f32), block(),
+            DMA((2, 8)), DMA((2, 2)), DMA((2, 8)), DMA((2, 8)), DMA((2, 8)),
+            DMA((1, 8)), DMA((1, 2)), DMA((1, 8)),
+            DMA((CHIPS,)), DMA((ENERGIES,)), DMA((ENERGIES,)), DMA((CHIPS,)), DMA((2,))],
+        compiler_params=pltpu.CompilerParams(vmem_limit_bytes=62 << 20, collective_id=0, has_side_effects=True),
+        name="born",
+    )(levels, offsets, phonon, onsite, coupling)
 
 
 def shards(onsite, coupling, phonon, levels, offsets):
-    green, coupling_all, onsite_all = first_round(levels, onsite, coupling)
-    combined = energy_sum(green, offsets)
-    green, self_energy = second_round(levels, phonon, combined, onsite_all, coupling_all)
+    green, self_energy = whole(levels, offsets, phonon, onsite, coupling)
     return green[None, None], self_energy[None, None]
 
 

time: 252 us -> 220 us (0.87); the launches traced: 248 us -> 219 us
  Pallas kernels: 177 us -> 215 us
  blocking collectives: 28.1 us -> 0 us
  waiting for transfers between devices: 15.8 us -> 0 us
  starting transfers between devices: 12.7 us -> 0 us
  local copies, waits for them, and re-layouts: 8.03 us -> 2.8 us
  between operations: 5.21 us -> 1.29 us
    pallas_call x2 -> x1, Pallas kernels: 177 us -> 215 us  [whole(): pl.pallas_call(whole_kernel, out_shape=(ONE, ONE), in_specs=[SM, SM, VM,...]
    all_to_all x1 -> x0, blocking collectives: 28.1 us -> none  [energy_sum(): return lax.all_to_all(combined, 'energy', 0, 0, tiled=True).reshape(NB, NB)]
    all_to_all x1 -> x0, waiting for transfers between devices: 15.8 us -> none  [energy_sum(): lax.all_to_all(green.reshape(count, rows, NB), 'energy', 0, 0, tiled=True)]
    all_to_all x1 -> x0, starting transfers between devices: 12.7 us -> none  [energy_sum(): lax.all_to_all(green.reshape(count, rows, NB), 'energy', 0, 0, tiled=True)]
    reshape x2 -> x0, local copies, waits for them, and re-layouts: 2.88 us -> none  [the longest x1 2 us: energy_sum(): green.reshape(count, rows, NB)]
  transfers between devices with their start and end apart: 1 -> 0, of which waited for: 1 -> 0; matrix products, arithmetic and copies ran while one was open for 1% -> 0% of each run, Pallas kernels for 0% -> 0%
where the time goes in v2:
time: 220 us; the launch traced here: 219 us
  Pallas kernels  215 us (98%)
  local copies, waits for them, and re-layouts  2.8 us (1%)
    pallas_call x1, Pallas kernels, whole(): pl.pallas_call(whole_kernel, out_shape=(ONE, ONE), in_specs=[SM, SM, VM,...  215 us

profile of v2, /device:TPU:15, one launch (start us, length us, event | category | flops | bytes accessed | tf_op | source)
XLA Modules:
  0.0 219.3 jit_solution(12416889539206150125)
XLA Ops:
  1.3 215.2 %born.1 = (f32[384,384]{1,0:T(8,128)}, f32[384,384]{1,0:T(8,128)}) custom-call(f32[1]{0:T(128)S(6)} %copy.9.lev_ref, s32[2]{0:T(128)} %off_ref.1, f32[1,384,384]{2,1,0:T(8,128)} %phi_ref.1, f32[1,384,384]{2,1,0:T(8,128)} %m_ref.1, f32[1,384,384]{2,1,0:T(8,128)} %c_ref.1), custom_call_target="tpu_custom_call" | custom-call | tf_op jit(solution)/shard_map/born/pallas_call | solution.py:388
  216.5 0.0 copy-start
  216.5 2.0 copy.10
  218.5 0.0 copy-done
  218.5 0.8 copy.11
Async XLA Ops:
  216.5 2.0 copy-start

commit v3 on v2

v3 whole, which is shorter than its diff:
```python
import functools
import jax
import jax.numpy as jnp
from jax import lax
from jax.experimental import pallas as pl
from jax.experimental.pallas import tpu as pltpu

NB = 384
SEGS = 8
ENERGIES = 32
CHIPS = ENERGIES // 2
SLAB = NB // CHIPS
PAD = 15
HALVES = 2
CUTS = 3
f32 = jnp.float32
bf16 = jnp.bfloat16
MESH = pl.DeviceIdType.MESH


def split(x):
    hi = x.astype(bf16)
    lo = (x - hi.astype(f32)).astype(bf16)
    return hi, lo


def put_left(ref, x):
    hi, lo = split(x)
    ref[:, 0:256] = hi[:, 0:256]
    ref[:, 256:512] = lo[:, 0:256]
    ref[:, 512:640] = hi[:, 256:384]
    ref[:, 640:768] = lo[:, 256:384]


def put_right(ref, x):
    hi, lo = split(x)
    ref[0:256, 0:384] = hi[0:256]
    ref[256:512, 0:384] = hi[0:256]
    ref[0:256, 384:768] = lo[0:256]
    ref[512:640, 0:384] = hi[256:384]
    ref[640:768, 0:384] = hi[256:384]
    ref[512:640, 384:768] = lo[256:384]


def clear_right(ref):
    ref[256:512, 384:768] = jnp.zeros((256, 384), bf16)
    ref[640:768, 384:768] = jnp.zeros((128, 384), bf16)


def dot(a, b):
    return lax.dot_general(a, b, (((1,), (0,)), ((), ())), preferred_element_type=f32)


def mm(l, r):
    out = []
    for h in range(HALVES):
        n = NB // HALVES
        rows = slice(h * n, h * n + n)
        a = dot(l[rows, :], r[:, 0:512])
        b = dot(l[rows, 0:256], r[0:256, 512:768]) + dot(l[rows, 512:768], r[512:768, 512:768])
        out.append(jnp.concatenate([a[:, 0:128] + a[:, 384:512], a[:, 128:384] + b], axis=1))
    return jnp.concatenate(out, axis=0)


def table(seg, values):
    out = jnp.int32(values[-1])
    for i, v in enumerate(values[:-1]):
        out = jnp.where(seg == i, jnp.int32(v), out)
    return out


class Gather:
    def __init__(self, parts, rsem, psem, ssem, dsem, dssem):
        self.parts, self.rsem, self.psem, self.ssem, self.dsem, self.dssem = parts, rsem, psem, ssem, dsem, dssem
        self.each = range(len(parts))
        self.twins = dsem is not None
        e = lax.axis_index("energy")
        self.seg = lax.axis_index("seg")
        self.sibling = {"energy": e + 1 - 2 * (e % 2)}
        self.pair, self.y = self.seg // 4, self.seg % 4
        at = lambda p, dy: p * 4 + (self.y + dy) % 4
        self.up, self.down, self.two = at(self.pair, 1), at(self.pair, 3), at(self.pair, 2)
        other = 1 - self.pair
        self.cross, self.cup, self.cdown, self.ctwo = at(other, 0), at(other, 1), at(other, 3), at(other, 2)

    def view(self, a, block, part=None):
        ref, base, n = self.parts[a]
        if part is not None:
            n = n // 2
            base = base + part * n
        return ref.at[block, pl.ds(pl.multiple_of(base, 8), n)]

    def copy(self, a, block, part, s, sem, to):
        ref = self.view(a, block, part)
        return pltpu.make_async_remote_copy(
            src_ref=ref, dst_ref=ref, send_sem=self.ssem.at[a, s], recv_sem=sem,
            device_id=to, device_id_type=MESH)

    def got(self, a, block, part=None):
        sem = self.rsem.at[a, block] if part is None else self.psem.at[a, part]
        self.copy(a, block, part, 0, sem, {"seg": self.up}).wait_recv()

    def send(self, a, i):
        r, p = self.rsem, self.psem
        up, down, cross = {"seg": self.up}, {"seg": self.down}, {"seg": self.cross}
        block, part, sem, to = (
            (self.seg, None, r.at[a, self.seg], up),
            (self.seg, None, r.at[a, self.seg], down),
            (self.seg, None, r.at[a, self.seg], cross),
            (self.down, 0, p.at[a, 0], up),
            (self.up, 1, p.at[a, 1], down),
            (self.cross, None, r.at[a, self.cross], up),
            (self.cross, None, r.at[a, self.cross], down),
            (self.two, None, r.at[a, self.two], cross),
        )[i]
        return self.copy(a, block, part, i, sem, to)

    def twin(self, a, block):
        ref = self.view(a, block)
        return pltpu.make_async_remote_copy(
            src_ref=ref, dst_ref=ref, send_sem=self.dssem.at[a, block], recv_sem=self.dsem.at[a, block],
            device_id=self.sibling, device_id_type=MESH)

    def pass_on(self, a, block):
        if self.twins:
            self.twin(a, block).start()

    def start(self, a):
        for i in range(3):
            self.send(a, i).start()

    def take(self, a, block, *sends):
        self.got(a, block)
        for i in sends:
            self.send(a, i).start()
        self.pass_on(a, block)

    def phase1(self):
        first = self.pair == 0

        @pl.when(first & (self.y == 1))
        def _():
            for a in self.each:
                self.take(a, self.up, 4)
            for a in self.each:
                self.take(a, self.cross, 6)
            for a in self.each:
                self.take(a, self.down, 3)
            for a in self.each:
                self.send(a, 5).start()

        @pl.when(first & (self.y == 3))
        def _():
            for a in self.each:
                self.take(a, self.down, 3)
            for a in self.each:
                self.take(a, self.cross, 5)
            for a in self.each:
                self.take(a, self.up, 4)
            for a in self.each:
                self.send(a, 6).start()

        @pl.when(jnp.logical_not(first & (self.y % 2 == 1)))
        def _():
            for a in self.each:
                self.take(a, self.down, 3)
                self.take(a, self.up, 4)
            for a in self.each:
                self.take(a, self.cross, 5, 6)

    def phase2(self):
        for a in self.each:
            self.got(a, self.two, 0)
            self.got(a, self.two, 1)
            self.send(a, 7).start()
            self.pass_on(a, self.two)

    def phase3(self):
        for a in self.each:
            for b in (self.cdown, self.cup):
                self.take(a, b)

    def phase4(self):
        for a in self.each:
            self.take(a, self.ctwo)

    def phases(self, k):
        for phase, times in ((self.phase1, (1, 0, 0, 0, 0, 0, 0, 0)), (self.phase2, (2, 3, 0, 1, 1, 0, 0, 0)),
                             (self.phase3, (5, 4, 4, 4, 1, 0, 0, 0)), (self.phase4, (6, 7, 4, 5, 2, 3, 0, 1))):
            pl.when(table(self.seg, times) == k)(phase)

    def need(self, a, k):
        @pl.when(k != self.seg)
        def _():
            ref, base, n = self.parts[a]
            other = ref.at[k, pl.ds(pl.multiple_of(n - base, 8), n)]
            pltpu.make_async_remote_copy(
                src_ref=other, dst_ref=other, send_sem=self.dssem.at[a, k], recv_sem=self.dsem.at[a, k],
                device_id=self.sibling, device_id_type=MESH).wait_recv()

    def finish(self):
        for a in self.each:
            for i in range(8):
                self.send(a, i).wait_send()
            if self.twins:
                for b in (self.down, self.up, self.cross, self.two, self.cdown, self.cup, self.ctwo):
                    self.twin(a, b).wait_send()


def entry_barrier():
    e = lax.axis_index("energy")
    seg = lax.axis_index("seg")
    core = e % 2
    pair, y = seg // 4, seg % 4
    barrier = pltpu.get_barrier_semaphore()

    def hello(to):
        pl.semaphore_signal(barrier, inc=1, device_id=to, device_id_type=MESH)

    for other in (pair * 4 + (y + 1) % 4, pair * 4 + (y + 3) % 4, (1 - pair) * 4 + y):
        hello({"seg": other})
    for d in range(1, 32):
        other = (e + d) % 32

        @pl.when((core == 1) | (other % 2 == 1))
        def _():
            hello({"energy": other})

    pl.semaphore_wait(barrier, 3 + 16 + 15 * core)


def identity():
    row = lax.broadcasted_iota(jnp.int32, (NB, NB), 0)
    col = lax.broadcasted_iota(jnp.int32, (NB, NB), 1)
    return (row == col).astype(f32)


def invert_into(L, s, x, el, rl, er, rr, br, fill=None):
    eye = identity()
    diag = x * eye
    d_col = 1.0 / jnp.sum(diag, axis=1, keepdims=True)
    d_row = 1.0 / jnp.sum(diag, axis=0, keepdims=True)
    e = eye - x * d_col
    put_left(el, e)
    put_right(er, e)
    if fill is not None:
        fill()
    r = mm(el, er)
    put_left(rl, r)
    put_right(rr, r)
    b = eye + e
    put_right(br, b)
    r = mm(rl, rr)
    b = b + mm(rl, br)
    put_left(el, r)
    put_right(er, r)
    put_right(br, b)
    r = mm(el, er)
    b = b + mm(el, br)
    put_left(rl, r)
    put_right(br, b)
    b = b + mm(rl, br)
    L[s] = b * d_row


def sweep(g, base_at, prepare, first, w, out):
    L, P, Q, C, CT, el, rl, er, rr, br, ql, ll = w
    seg = lax.axis_index("seg")
    g.phases(0)
    prepare(0)
    invert_into(L, 0, first(), el, rl, er, rr, br)

    def forward(k, carry):
        g.phases(k)
        prepare(k)
        left = L[k - 1]
        put_right(br, left)
        put_left(ll, left)
        q = mm(C.at[k], br)
        put_left(ql, q)
        put_right(Q.at[k], q)
        x = base_at(k) - mm(ql, CT.at[k])

        def fill():
            put_left(P.at[k], mm(ll, CT.at[k]))

        invert_into(L, k, x, el, rl, er, rr, br, fill)
        return carry

    lax.fori_loop(1, SEGS, forward, 0)
    out[...] = L[SEGS - 1]

    def backward(i, carry):
        t = SEGS - 1 - i
        put_right(br, out[...])
        put_left(el, mm(P.at[t], br))
        out[...] = L[t - 1] + mm(el, Q.at[t])
        return carry

    lax.fori_loop(0, SEGS - 1 - seg, backward, 0)


def exchange(green, off_ref, got, slabs, combined, out_ssem, out_rsem, back_ssem, back_rsem, meanwhile):
    e = lax.axis_index("energy")
    core, chip = e % 2, e // 2
    adder = core == 1

    def slab_rows(j):
        return pl.ds(pl.multiple_of(j * SLAB, 8), SLAB)

    def out_copy(j, source):
        return pltpu.make_async_remote_copy(
            src_ref=green.at[slab_rows(j)], dst_ref=got.at[PAD + source], send_sem=out_ssem.at[j], recv_sem=out_rsem.at[source],
            device_id={"energy": 2 * j + 1}, device_id_type=MESH)

    def back_copy(energy, j):
        return pltpu.make_async_remote_copy(
            src_ref=slabs.at[energy], dst_ref=combined.at[slab_rows(j)], send_sem=back_ssem.at[energy], recv_sem=back_rsem.at[j],
            device_id={"energy": energy}, device_id_type=MESH)

    def send_out(d, carry):
        j = (chip + d) % CHIPS

        @pl.when(e != 2 * j + 1)
        def _():
            out_copy(j, e).start()
        return carry

    lax.fori_loop(0, CHIPS, send_out, 0)
    meanwhile()

    @pl.when(adder)
    def _():
        got[PAD + e] = green[slab_rows(chip)]
        edge = jnp.zeros((SLAB, NB), f32)
        for i in range(PAD):
            got[i] = edge
            got[PAD + ENERGIES + i] = edge

        def receive(d, carry):
            source = (e + d) % ENERGIES
            out_copy(chip, source).wait_recv()
            return carry

        lax.fori_loop(1, ENERGIES, receive, 0)
        o1, o2 = off_ref[0], off_ref[1]

        def add(i, carry):
            p = PAD + i
            slabs[i] = got[p - o1] + got[p - o2] + got[p + o1] + got[p + o2]
            return carry

        lax.fori_loop(0, ENERGIES, add, 0)
        combined[slab_rows(chip)] = slabs[e]

        def send_back(d, carry):
            back_copy((e + d) % ENERGIES, chip).start()
            return carry

        lax.fori_loop(1, ENERGIES, send_back, 0)

    def receive_back(j, carry):
        @pl.when(e != 2 * j + 1)
        def _():
            back_copy(e, j).wait_recv()
        return carry

    lax.fori_loop(0, CHIPS, receive_back, 0)

    def finish():
        def sent_out(j, carry):
            @pl.when(e != 2 * j + 1)
            def _():
                out_copy(j, e).wait_send()
            return carry

        lax.fori_loop(0, CHIPS, sent_out, 0)

        @pl.when(adder)
        def _():
            def sent_back(d, carry):
                back_copy((e + d) % ENERGIES, chip).wait_send()
                return carry

            lax.fori_loop(1, ENERGIES, sent_back, 0)

    return finish


def whole_kernel(lev_ref, off_ref, phi_ref, m_ref, c_ref, o_ref, se_ref,
                 cb, mb, sb, L, P, Q, C, CT, el, rl, er, rr, br, ql, ll, base0, green, got, slabs, combined,
                 rsem, psem, ssem, dsem, dssem, rsem2, psem2, ssem2, out_ssem, out_rsem, back_ssem, back_rsem, lsem):
    seg = lax.axis_index("seg")
    own = [pltpu.make_async_copy(c_ref.at[0], cb.at[seg], lsem.at[0]),
           pltpu.make_async_copy(m_ref.at[0], mb.at[seg], lsem.at[1])]
    for c in own:
        c.start()
    entry_barrier()
    half = NB // 2
    mine = (lax.axis_index("energy") % 2) * half
    g = Gather(((cb, mine, half), (mb, mine, half)), rsem, psem, ssem, dsem, dssem)
    for a, c in enumerate(own):
        c.wait()
        g.start(a)
    for ref in (er, rr, br):
        clear_right(ref)
    w = (L, P, Q, C, CT, el, rl, er, rr, br, ql, ll)

    def prepare(k):
        clear_right(CT.at[k])
        clear_right(Q.at[k])
        g.need(0, k)
        g.need(1, k)
        c = cb[k]
        put_left(C.at[k], c)
        put_right(CT.at[k], c.T)

    def base_at(k):
        return mb[k] + lev_ref[0] * identity()

    def first():
        x = base_at(0) - 0.25 * mm(C.at[0], CT.at[0])
        base0[...] = x
        return x

    sweep(g, base_at, prepare, first, w, green)

    def meanwhile():
        phi = phi_ref[0]
        put_left(el, phi)
        put_right(rr, phi.T)

    finish = exchange(green, off_ref, got, slabs, combined, out_ssem, out_rsem, back_ssem, back_rsem, meanwhile)
    put_right(br, combined[...])
    put_left(ql, mm(el, br))
    sb[seg] = mm(ql, rr)
    third = NB // CUTS
    g2 = Gather([(sb, a * third, third) for a in range(CUTS)], rsem2, psem2, ssem2, None, None)
    for a in range(CUTS):
        g2.start(a)
    se_ref[...] = sb[seg]
    sweep(g2, lambda k: base_at(k) + sb[k], lambda k: None, lambda: base0[...] + sb[0], w, o_ref)
    finish()
    g.finish()
    g2.finish()


def block(n=None):
    return pltpu.VMEM((NB, NB) if n is None else (n, NB, NB), f32)


def left(*n):
    return pltpu.VMEM((*n, NB, 2 * NB), bf16)


def right(*n):
    return pltpu.VMEM((*n, 2 * NB, 2 * NB), bf16)


WORK = [block(8), left(8), right(8), left(8), right(8), left(), left(), right(), right(), right(), left(), left(), block()]
DMA = pltpu.SemaphoreType.DMA
VM = pl.BlockSpec(memory_space=pltpu.VMEM)
SM = pl.BlockSpec(memory_space=pltpu.SMEM)
ANY = pl.BlockSpec(memory_space=pl.ANY)
ONE = jax.ShapeDtypeStruct((NB, NB), f32)


def whole(levels, offsets, phonon, onsite, coupling):
    return pl.pallas_call(
        whole_kernel, out_shape=(ONE, ONE),
        in_specs=[SM, SM, VM, ANY, ANY], out_specs=(VM, VM),
        scratch_shapes=[block(8), block(8), block(8)] + WORK + [
            block(), pltpu.VMEM((ENERGIES + 2 * PAD, SLAB, NB), f32), pltpu.VMEM((ENERGIES, SLAB, NB), f32), block(),
            DMA((2, 8)), DMA((2, 2)), DMA((2, 8)), DMA((2, 8)), DMA((2, 8)),
            DMA((CUTS, 8)), DMA((CUTS, 2)), DMA((CUTS, 8)),
            DMA((CHIPS,)), DMA((ENERGIES,)), DMA((ENERGIES,)), DMA((CHIPS,)), DMA((2,))],
        compiler_params=pltpu.CompilerParams(vmem_limit_bytes=62 << 20, collective_id=0, has_side_effects=True),
        name="born",
    )(levels, offsets, phonon, onsite, coupling)


def shards(onsite, coupling, phonon, levels, offsets):
    green, self_energy = whole(levels, offsets, phonon, onsite, coupling)
    return green[None, None], self_energy[None, None]


def solution(mesh):
    spec = jax.sharding.PartitionSpec
    block_in = spec("seg", None, None)
    block_out = spec("energy", "seg", None, None)
    return jax.shard_map(shards, mesh=mesh, in_specs=(block_in, block_in, block_in, spec("energy"), spec()),
                         out_specs=(block_out, block_out), check_vma=False)
```

time: 220 us -> 194 us (0.88)
  Pallas kernels: 215 us -> 190 us
    pallas_call x1, Pallas kernels: 215 us -> 190 us  [whole(): pl.pallas_call(whole_kernel, out_shape=(ONE, ONE), in_specs=[SM, SM, VM,...]
where the time goes in v3:
time: 194 us
  Pallas kernels  190 us (98%)
  local copies, waits for them, and re-layouts  2.8 us (1%)
    pallas_call x1, Pallas kernels, whole(): pl.pallas_call(whole_kernel, out_shape=(ONE, ONE), in_specs=[SM, SM, VM,...  190 us

profile of v3, /device:TPU:15, one launch (start us, length us, event | category | flops | bytes accessed | tf_op | source)
XLA Modules:
  0.0 194.1 jit_solution(11285878732987751157)
XLA Ops:
  1.3 190.1 %born.1 = (f32[384,384]{1,0:T(8,128)}, f32[384,384]{1,0:T(8,128)}) custom-call(f32[1]{0:T(128)S(6)} %copy.9.lev_ref, s32[2]{0:T(128)} %off_ref.1, f32[1,384,384]{2,1,0:T(8,128)} %phi_ref.1, f32[1,384,384]{2,1,0:T(8,128)} %m_ref.1, f32[1,384,384]{2,1,0:T(8,128)} %c_ref.1), custom_call_target="tpu_custom_call" | custom-call | tf_op jit(solution)/shard_map/born/pallas_call | solution.py:469
  191.3 0.0 copy-start
  191.3 2.0 %copy.10 = f32[1,1,384,384]{3,2,1,0:T(8,128)} copy(f32[1,1,384,384]{3,2,1,0:T(8,128)} %bitcast.3) | data formatting | bytes 1179648
  193.3 0.0 copy-done
  193.3 0.8 copy.11
Async XLA Ops:
  191.3 2.0 %copy-start = (f32[384,384]{1,0:T(8,128)S(1)}, f32[384,384]{1,0:T(8,128)}, u32[]{:S(2)}) copy-start(f32[384,384]{1,0:T(8,128)} %get-tuple-element.5) | copy-start | bytes 1769476

commit v4 on v3

--- a/solution.py
+++ b/solution.py
@@ -12,7 +12,8 @@
 SLAB = NB // CHIPS
 PAD = 15
 HALVES = 2
-CUTS = 3
+CUTS = 6
+PARTS = 3
 f32 = jnp.float32
 bf16 = jnp.bfloat16
 MESH = pl.DeviceIdType.MESH
@@ -96,8 +97,8 @@
             src_ref=ref, dst_ref=ref, send_sem=self.ssem.at[a, s], recv_sem=sem,
             device_id=to, device_id_type=MESH)
 
-    def got(self, a, block, part=None):
-        sem = self.rsem.at[a, block] if part is None else self.psem.at[a, part]
+    def got(self, a, block, part=None, base=0):
+        sem = self.rsem.at[a, block] if part is None else self.psem.at[a, base + part]
         self.copy(a, block, part, 0, sem, {"seg": self.up}).wait_recv()
 
     def send(self, a, i):
@@ -112,6 +113,8 @@
             (self.cross, None, r.at[a, self.cross], up),
             (self.cross, None, r.at[a, self.cross], down),
             (self.two, None, r.at[a, self.two], cross),
+            (self.cdown, 0, p.at[a, 2], up),
+            (self.cup, 1, p.at[a, 3], down),
         )[i]
         return self.copy(a, block, part, i, sem, to)
 
@@ -135,10 +138,8 @@
             self.send(a, i).start()
         self.pass_on(a, block)
 
-    def phase1(self):
-        first = self.pair == 0
-
-        @pl.when(first & (self.y == 1))
+    def first_column_near(self):
+        @pl.when(self.y == 1)
         def _():
             for a in self.each:
                 self.take(a, self.up, 4)
@@ -149,7 +150,7 @@
             for a in self.each:
                 self.send(a, 5).start()
 
-        @pl.when(first & (self.y == 3))
+        @pl.when(self.y == 3)
         def _():
             for a in self.each:
                 self.take(a, self.down, 3)
@@ -160,7 +161,7 @@
             for a in self.each:
                 self.send(a, 6).start()
 
-        @pl.when(jnp.logical_not(first & (self.y % 2 == 1)))
+        @pl.when(self.y % 2 == 0)
         def _():
             for a in self.each:
                 self.take(a, self.down, 3)
@@ -168,25 +169,57 @@
             for a in self.each:
                 self.take(a, self.cross, 5, 6)
 
-    def phase2(self):
+    def first_column_two(self):
+        for a in self.each:
+            self.got(a, self.two, 0)
+            self.got(a, self.two, 1)
+            self.pass_on(a, self.two)
+
+    def first_column_cross(self):
+        for a in self.each:
+            self.take(a, self.cdown)
+            self.take(a, self.cup)
+
+    def first_column_far(self):
+        for a in self.each:
+            self.take(a, self.ctwo)
+
+    def second_column(self):
+        for a in self.each:
+            self.take(a, self.down, 3)
+            self.take(a, self.up, 4)
+        for a in self.each:
+            self.take(a, self.cross, 5, 6)
         for a in self.each:
             self.got(a, self.two, 0)
             self.got(a, self.two, 1)
             self.send(a, 7).start()
             self.pass_on(a, self.two)
 
-    def phase3(self):
-        for a in self.each:
-            for b in (self.cdown, self.cup):
-                self.take(a, b)
-
-    def phase4(self):
-        for a in self.each:
-            self.take(a, self.ctwo)
+        @pl.when(self.y == 1)
+        def _():
+            for a in self.each:
+                self.take(a, self.cup, 9)
+            for a in self.each:
+                self.take(a, self.cdown, 8)
+
+        @pl.when(self.y != 1)
+        def _():
+            for a in self.each:
+                self.take(a, self.cdown, 8)
+            for a in self.each:
+                self.take(a, self.cup, 9)
+
+    def second_column_far(self):
+        for a in self.each:
+            self.got(a, self.ctwo, 0, 2)
+            self.got(a, self.ctwo, 1, 2)
+            self.pass_on(a, self.ctwo)
 
     def phases(self, k):
-        for phase, times in ((self.phase1, (1, 0, 0, 0, 0, 0, 0, 0)), (self.phase2, (2, 3, 0, 1, 1, 0, 0, 0)),
-                             (self.phase3, (5, 4, 4, 4, 1, 0, 0, 0)), (self.phase4, (6, 7, 4, 5, 2, 3, 0, 1))):
+        for phase, times in ((self.first_column_near, (1, 0, 0, 0, 9, 9, 9, 9)), (self.first_column_two, (2, 3, 0, 1, 9, 9, 9, 9)),
+                             (self.first_column_cross, (5, 4, 4, 4, 9, 9, 9, 9)), (self.first_column_far, (6, 7, 4, 5, 9, 9, 9, 9)),
+                             (self.second_column, (9, 9, 9, 9, 0, 0, 0, 0)), (self.second_column_far, (9, 9, 9, 9, 2, 3, 0, 1))):
             pl.when(table(self.seg, times) == k)(phase)
 
     def need(self, a, k):
@@ -200,8 +233,13 @@
 
     def finish(self):
         for a in self.each:
-            for i in range(8):
+            for i in range(7):
                 self.send(a, i).wait_send()
+
+            @pl.when(self.pair == 1)
+            def _():
+                for i in (7, 8, 9):
+                    self.send(a, i).wait_send()
             if self.twins:
                 for b in (self.down, self.up, self.cross, self.two, self.cdown, self.cup, self.ctwo):
                     self.twin(a, b).wait_send()
@@ -305,90 +343,89 @@
     core, chip = e % 2, e // 2
     adder = core == 1
 
-    def slab_rows(j):
-        return pl.ds(pl.multiple_of(j * SLAB, 8), SLAB)
-
-    def out_copy(j, source):
+    rows = SLAB // PARTS
+
+    def at(j, p):
+        return pl.ds(pl.multiple_of(j * SLAB + p * rows, 8), rows)
+
+    def out_copy(j, source, p):
         return pltpu.make_async_remote_copy(
-            src_ref=green.at[slab_rows(j)], dst_ref=got.at[PAD + source], send_sem=out_ssem.at[j], recv_sem=out_rsem.at[source],
+            src_ref=green.at[at(j, p)], dst_ref=got[p].at[PAD + source],
+            send_sem=out_ssem.at[p, j], recv_sem=out_rsem.at[p, source],
             device_id={"energy": 2 * j + 1}, device_id_type=MESH)
 
-    def back_copy(energy, j):
+    def back_copy(energy, j, p):
         return pltpu.make_async_remote_copy(
-            src_ref=slabs.at[energy], dst_ref=combined.at[slab_rows(j)], send_sem=back_ssem.at[energy], recv_sem=back_rsem.at[j],
+            src_ref=slabs.at[energy, at(0, p)], dst_ref=combined.at[at(j, p)],
+            send_sem=back_ssem.at[p, energy], recv_sem=back_rsem.at[p, j],
             device_id={"energy": energy}, device_id_type=MESH)
 
-    def send_out(d, carry):
-        j = (chip + d) % CHIPS
-
-        @pl.when(e != 2 * j + 1)
-        def _():
-            out_copy(j, e).start()
-        return carry
-
-    lax.fori_loop(0, CHIPS, send_out, 0)
+    def for_chips(body):
+        for p in range(PARTS):
+            def one(d, carry):
+                j = (chip + d) % CHIPS
+
+                @pl.when(e != 2 * j + 1)
+                def _():
+                    body(j, p)
+                return carry
+            lax.fori_loop(0, CHIPS, one, 0)
+
+    for_chips(lambda j, p: out_copy(j, e, p).start())
     meanwhile()
 
     @pl.when(adder)
     def _():
-        got[PAD + e] = green[slab_rows(chip)]
-        edge = jnp.zeros((SLAB, NB), f32)
-        for i in range(PAD):
-            got[i] = edge
-            got[PAD + ENERGIES + i] = edge
-
-        def receive(d, carry):
-            source = (e + d) % ENERGIES
-            out_copy(chip, source).wait_recv()
-            return carry
-
-        lax.fori_loop(1, ENERGIES, receive, 0)
+        mine = pl.ds(pl.multiple_of(chip * SLAB, 8), SLAB)
+        edge = jnp.zeros((rows, NB), f32)
+        for p in range(PARTS):
+            got[p][PAD + e] = green[at(chip, p)]
+            for i in range(PAD):
+                got[p][i] = edge
+                got[p][PAD + ENERGIES + i] = edge
         o1, o2 = off_ref[0], off_ref[1]
-
-        def add(i, carry):
-            p = PAD + i
-            slabs[i] = got[p - o1] + got[p - o2] + got[p + o1] + got[p + o2]
-            return carry
-
-        lax.fori_loop(0, ENERGIES, add, 0)
-        combined[slab_rows(chip)] = slabs[e]
-
-        def send_back(d, carry):
-            back_copy((e + d) % ENERGIES, chip).start()
-            return carry
-
-        lax.fori_loop(1, ENERGIES, send_back, 0)
-
-    def receive_back(j, carry):
-        @pl.when(e != 2 * j + 1)
-        def _():
-            back_copy(e, j).wait_recv()
-        return carry
-
-    lax.fori_loop(0, CHIPS, receive_back, 0)
+        for p in range(PARTS):
+            piece = pl.ds(p * rows, rows)
+
+            def receive(d, carry):
+                out_copy(chip, (e + d) % ENERGIES, p).wait_recv()
+                return carry
+
+            lax.fori_loop(1, ENERGIES, receive, 0)
+
+            def add(i, carry):
+                c = PAD + i
+                slabs[i, piece] = got[p][c - o1] + got[p][c - o2] + got[p][c + o1] + got[p][c + o2]
+                return carry
+
+            lax.fori_loop(0, ENERGIES, add, 0)
+
+            def send_back(d, carry):
+                back_copy((e + d) % ENERGIES, chip, p).start()
+                return carry
+
+            lax.fori_loop(1, ENERGIES, send_back, 0)
+        combined[mine] = slabs[e]
+
+    for_chips(lambda j, p: back_copy(e, j, p).wait_recv())
 
     def finish():
-        def sent_out(j, carry):
-            @pl.when(e != 2 * j + 1)
-            def _():
-                out_copy(j, e).wait_send()
-            return carry
-
-        lax.fori_loop(0, CHIPS, sent_out, 0)
+        for_chips(lambda j, p: out_copy(j, e, p).wait_send())
 
         @pl.when(adder)
         def _():
-            def sent_back(d, carry):
-                back_copy((e + d) % ENERGIES, chip).wait_send()
-                return carry
-
-            lax.fori_loop(1, ENERGIES, sent_back, 0)
+            for p in range(PARTS):
+                def sent_back(d, carry):
+                    back_copy((e + d) % ENERGIES, chip, p).wait_send()
+                    return carry
+
+                lax.fori_loop(1, ENERGIES, sent_back, 0)
 
     return finish
 
 
 def whole_kernel(lev_ref, off_ref, phi_ref, m_ref, c_ref, o_ref, se_ref,
-                 cb, mb, sb, L, P, Q, C, CT, el, rl, er, rr, br, ql, ll, base0, green, got, slabs, combined,
+                 cb, mb, sb, L, P, Q, C, CT, el, rl, er, rr, br, ql, ll, base0, green, got0, got1, got2, slabs, combined,
                  rsem, psem, ssem, dsem, dssem, rsem2, psem2, ssem2, out_ssem, out_rsem, back_ssem, back_rsem, lsem):
     seg = lax.axis_index("seg")
     own = [pltpu.make_async_copy(c_ref.at[0], cb.at[seg], lsem.at[0]),
@@ -430,7 +467,7 @@
         put_left(el, phi)
         put_right(rr, phi.T)
 
-    finish = exchange(green, off_ref, got, slabs, combined, out_ssem, out_rsem, back_ssem, back_rsem, meanwhile)
+    finish = exchange(green, off_ref, (got0, got1, got2), slabs, combined, out_ssem, out_rsem, back_ssem, back_rsem, meanwhile)
     put_right(br, combined[...])
     put_left(ql, mm(el, br))
     sb[seg] = mm(ql, rr)
@@ -470,10 +507,10 @@
         whole_kernel, out_shape=(ONE, ONE),
         in_specs=[SM, SM, VM, ANY, ANY], out_specs=(VM, VM),
         scratch_shapes=[block(8), block(8), block(8)] + WORK + [
-            block(), pltpu.VMEM((ENERGIES + 2 * PAD, SLAB, NB), f32), pltpu.VMEM((ENERGIES, SLAB, NB), f32), block(),
-            DMA((2, 8)), DMA((2, 2)), DMA((2, 8)), DMA((2, 8)), DMA((2, 8)),
-            DMA((CUTS, 8)), DMA((CUTS, 2)), DMA((CUTS, 8)),
-            DMA((CHIPS,)), DMA((ENERGIES,)), DMA((ENERGIES,)), DMA((CHIPS,)), DMA((2,))],
+            block(), *[pltpu.VMEM((ENERGIES + 2 * PAD, SLAB // PARTS, NB), f32)] * PARTS, pltpu.VMEM((ENERGIES, SLAB, NB), f32), block(),
+            DMA((2, 8)), DMA((2, 4)), DMA((2, 10)), DMA((2, 8)), DMA((2, 8)),
+            DMA((CUTS, 8)), DMA((CUTS, 4)), DMA((CUTS, 10)),
+            DMA((PARTS, CHIPS)), DMA((PARTS, ENERGIES)), DMA((PARTS, ENERGIES)), DMA((PARTS, CHIPS)), DMA((2,))],
         compiler_params=pltpu.CompilerParams(vmem_limit_bytes=62 << 20, collective_id=0, has_side_effects=True),
         name="born",
     )(levels, offsets, phonon, onsite, coupling)

time: 194 us -> 205 us (1.057)
  the two profiles are of different devices: /device:TPU:15 before, /device:TPU:19 now
where the time goes in v4:
time: 205 us
  Pallas kernels  201 us (98%)
  local copies, waits for them, and re-layouts  2.8 us (1%)
    pallas_call x1, Pallas kernels, whole(): pl.pallas_call(whole_kernel, out_shape=(ONE, ONE), in_specs=[SM, SM, VM,...  201 us

profile of v4, /device:TPU:19, one launch (start us, length us, event | category | flops | bytes accessed | tf_op | source)
XLA Modules:
  0.0 205.3 jit_solution(8586340759704150634)
XLA Ops:
  1.3 201.2 %born.1 = (f32[384,384]{1,0:T(8,128)}, f32[384,384]{1,0:T(8,128)}) custom-call(f32[1]{0:T(128)S(6)} %copy.9.lev_ref, s32[2]{0:T(128)} %off_ref.1, f32[1,384,384]{2,1,0:T(8,128)} %phi_ref.1, f32[1,384,384]{2,1,0:T(8,128)} %m_ref.1, f32[1,384,384]{2,1,0:T(8,128)} %c_ref.1), custom_call_target="tpu_custom_call" | custom-call | tf_op jit(solution)/shard_map/born/pallas_call | solution.py:506
  202.5 0.0 copy-start
  202.5 2.0 copy.10
  204.5 0.0 copy-done
  204.5 0.8 copy.11
Async XLA Ops:
  202.5 2.0 copy-start

commit v5 on v4

--- a/solution.py
+++ b/solution.py
@@ -11,9 +11,11 @@
 CHIPS = ENERGIES // 2
 SLAB = NB // CHIPS
 PAD = 15
+PARTS = 3
+RING = 8
+ORDER = (12, 4, 11, 13, 3, 5, 10, 14, 2, 6, 9, 15, 1, 7, 8, 0)
 HALVES = 2
-CUTS = 6
-PARTS = 3
+CUTS = 3
 f32 = jnp.float32
 bf16 = jnp.bfloat16
 MESH = pl.DeviceIdType.MESH
@@ -52,9 +54,9 @@
     return lax.dot_general(a, b, (((1,), (0,)), ((), ())), preferred_element_type=f32)
 
 
-def mm(l, r):
+def mm(l, r, which=None):
     out = []
-    for h in range(HALVES):
+    for h in range(HALVES) if which is None else (which,):
         n = NB // HALVES
         rows = slice(h * n, h * n + n)
         a = dot(l[rows, :], r[:, 0:512])
@@ -97,8 +99,8 @@
             src_ref=ref, dst_ref=ref, send_sem=self.ssem.at[a, s], recv_sem=sem,
             device_id=to, device_id_type=MESH)
 
-    def got(self, a, block, part=None, base=0):
-        sem = self.rsem.at[a, block] if part is None else self.psem.at[a, base + part]
+    def got(self, a, block, part=None):
+        sem = self.rsem.at[a, block] if part is None else self.psem.at[a, part]
         self.copy(a, block, part, 0, sem, {"seg": self.up}).wait_recv()
 
     def send(self, a, i):
@@ -113,8 +115,6 @@
             (self.cross, None, r.at[a, self.cross], up),
             (self.cross, None, r.at[a, self.cross], down),
             (self.two, None, r.at[a, self.two], cross),
-            (self.cdown, 0, p.at[a, 2], up),
-            (self.cup, 1, p.at[a, 3], down),
         )[i]
         return self.copy(a, block, part, i, sem, to)
 
@@ -138,88 +138,32 @@
             self.send(a, i).start()
         self.pass_on(a, block)
 
-    def first_column_near(self):
-        @pl.when(self.y == 1)
-        def _():
-            for a in self.each:
-                self.take(a, self.up, 4)
-            for a in self.each:
-                self.take(a, self.cross, 6)
-            for a in self.each:
-                self.take(a, self.down, 3)
-            for a in self.each:
-                self.send(a, 5).start()
-
-        @pl.when(self.y == 3)
-        def _():
-            for a in self.each:
-                self.take(a, self.down, 3)
-            for a in self.each:
-                self.take(a, self.cross, 5)
-            for a in self.each:
-                self.take(a, self.up, 4)
-            for a in self.each:
-                self.send(a, 6).start()
-
-        @pl.when(self.y % 2 == 0)
-        def _():
-            for a in self.each:
-                self.take(a, self.down, 3)
-                self.take(a, self.up, 4)
-            for a in self.each:
-                self.take(a, self.cross, 5, 6)
-
-    def first_column_two(self):
-        for a in self.each:
-            self.got(a, self.two, 0)
-            self.got(a, self.two, 1)
-            self.pass_on(a, self.two)
-
-    def first_column_cross(self):
-        for a in self.each:
-            self.take(a, self.cdown)
-            self.take(a, self.cup)
-
-    def first_column_far(self):
-        for a in self.each:
-            self.take(a, self.ctwo)
-
-    def second_column(self):
+    def phase1(self):
         for a in self.each:
             self.take(a, self.down, 3)
             self.take(a, self.up, 4)
         for a in self.each:
             self.take(a, self.cross, 5, 6)
+
+    def phase2(self):
         for a in self.each:
             self.got(a, self.two, 0)
             self.got(a, self.two, 1)
             self.send(a, 7).start()
             self.pass_on(a, self.two)
 
-        @pl.when(self.y == 1)
-        def _():
-            for a in self.each:
-                self.take(a, self.cup, 9)
-            for a in self.each:
-                self.take(a, self.cdown, 8)
-
-        @pl.when(self.y != 1)
-        def _():
-            for a in self.each:
-                self.take(a, self.cdown, 8)
-            for a in self.each:
-                self.take(a, self.cup, 9)
-
-    def second_column_far(self):
-        for a in self.each:
-            self.got(a, self.ctwo, 0, 2)
-            self.got(a, self.ctwo, 1, 2)
-            self.pass_on(a, self.ctwo)
+    def phase3(self):
+        for a in self.each:
+            for b in (self.cdown, self.cup):
+                self.take(a, b)
+
+    def phase4(self):
+        for a in self.each:
+            self.take(a, self.ctwo)
 
     def phases(self, k):
-        for phase, times in ((self.first_column_near, (1, 0, 0, 0, 9, 9, 9, 9)), (self.first_column_two, (2, 3, 0, 1, 9, 9, 9, 9)),
-                             (self.first_column_cross, (5, 4, 4, 4, 9, 9, 9, 9)), (self.first_column_far, (6, 7, 4, 5, 9, 9, 9, 9)),
-                             (self.second_column, (9, 9, 9, 9, 0, 0, 0, 0)), (self.second_column_far, (9, 9, 9, 9, 2, 3, 0, 1))):
+        for phase, times in ((self.phase1, (1, 0, 0, 0, 0, 0, 0, 0)), (self.phase2, (2, 3, 0, 1, 1, 0, 0, 0)),
+                             (self.phase3, (5, 4, 4, 4, 1, 0, 0, 0)), (self.phase4, (6, 7, 4, 5, 2, 3, 0, 1))):
             pl.when(table(self.seg, times) == k)(phase)
 
     def need(self, a, k):
@@ -233,13 +177,8 @@
 
     def finish(self):
         for a in self.each:
-            for i in range(7):
+            for i in range(8):
                 self.send(a, i).wait_send()
-
-            @pl.when(self.pair == 1)
-            def _():
-                for i in (7, 8, 9):
-                    self.send(a, i).wait_send()
             if self.twins:
                 for b in (self.down, self.up, self.cross, self.two, self.cdown, self.cup, self.ctwo):
                     self.twin(a, b).wait_send()
@@ -282,8 +221,10 @@
     put_left(el, e)
     put_right(er, e)
     if fill is not None:
-        fill()
+        fill(0)
     r = mm(el, er)
+    if fill is not None:
+        fill(1)
     put_left(rl, r)
     put_right(rr, r)
     b = eye + e
@@ -319,8 +260,8 @@
         put_right(Q.at[k], q)
         x = base_at(k) - mm(ql, CT.at[k])
 
-        def fill():
-            put_left(P.at[k], mm(ll, CT.at[k]))
+        def fill(h):
+            put_left(P.at[k, pl.ds(h * (NB // HALVES), NB // HALVES)], mm(ll, CT.at[k], h))
 
         invert_into(L, k, x, el, rl, er, rr, br, fill)
         return carry
@@ -360,16 +301,17 @@
             send_sem=back_ssem.at[p, energy], recv_sem=back_rsem.at[p, j],
             device_id={"energy": energy}, device_id_type=MESH)
 
+    def chip_at(d):
+        return (chip // RING + d // RING) % 2 * RING + (chip + d) % RING
+
     def for_chips(body):
         for p in range(PARTS):
-            def one(d, carry):
-                j = (chip + d) % CHIPS
+            for d in ORDER:
+                j = chip_at(d)
 
                 @pl.when(e != 2 * j + 1)
                 def _():
                     body(j, p)
-                return carry
-            lax.fori_loop(0, CHIPS, one, 0)
 
     for_chips(lambda j, p: out_copy(j, e, p).start())
     meanwhile()
@@ -400,11 +342,10 @@
 
             lax.fori_loop(0, ENERGIES, add, 0)
 
-            def send_back(d, carry):
-                back_copy((e + d) % ENERGIES, chip, p).start()
-                return carry
-
-            lax.fori_loop(1, ENERGIES, send_back, 0)
+            for d in ORDER:
+                back_copy(2 * chip_at(d), chip, p).start()
+                if d:
+                    back_copy(2 * chip_at(d) + 1, chip, p).start()
         combined[mine] = slabs[e]
 
     for_chips(lambda j, p: back_copy(e, j, p).wait_recv())
@@ -508,8 +449,8 @@
         in_specs=[SM, SM, VM, ANY, ANY], out_specs=(VM, VM),
         scratch_shapes=[block(8), block(8), block(8)] + WORK + [
             block(), *[pltpu.VMEM((ENERGIES + 2 * PAD, SLAB // PARTS, NB), f32)] * PARTS, pltpu.VMEM((ENERGIES, SLAB, NB), f32), block(),
-            DMA((2, 8)), DMA((2, 4)), DMA((2, 10)), DMA((2, 8)), DMA((2, 8)),
-            DMA((CUTS, 8)), DMA((CUTS, 4)), DMA((CUTS, 10)),
+            DMA((2, 8)), DMA((2, 2)), DMA((2, 8)), DMA((2, 8)), DMA((2, 8)),
+            DMA((CUTS, 8)), DMA((CUTS, 2)), DMA((CUTS, 8)),
             DMA((PARTS, CHIPS)), DMA((PARTS, ENERGIES)), DMA((PARTS, ENERGIES)), DMA((PARTS, CHIPS)), DMA((2,))],
         compiler_params=pltpu.CompilerParams(vmem_limit_bytes=62 << 20, collective_id=0, has_side_effects=True),
         name="born",

time: 205 us -> 191 us (0.932)
  the two profiles are of different devices: /device:TPU:19 before, /device:TPU:15 now
where the time goes in v5:
time: 191 us
  Pallas kernels  187 us (98%)
  local copies, waits for them, and re-layouts  2.8 us (1%)
    pallas_call x1, Pallas kernels, whole(): pl.pallas_call(whole_kernel, out_shape=(ONE, ONE), in_specs=[SM, SM, VM,...  187 us

profile of v5, /device:TPU:15, one launch (start us, length us, event | category | flops | bytes accessed | tf_op | source)
XLA Modules:
  0.0 190.8 jit_solution(2521756293839470058)
XLA Ops:
  1.3 186.7 %born.1 = (f32[384,384]{1,0:T(8,128)}, f32[384,384]{1,0:T(8,128)}) custom-call(f32[1]{0:T(128)S(6)} %copy.9.lev_ref, s32[2]{0:T(128)} %off_ref.1, f32[1,384,384]{2,1,0:T(8,128)} %phi_ref.1, f32[1,384,384]{2,1,0:T(8,128)} %m_ref.1, f32[1,384,384]{2,1,0:T(8,128)} %c_ref.1), custom_call_target="tpu_custom_call" | custom-call | tf_op jit(solution)/shard_map/born/pallas_call | solution.py:447
  188.0 0.0 copy-start
  188.0 2.0 %copy.10 = f32[1,1,384,384]{3,2,1,0:T(8,128)} copy(f32[1,1,384,384]{3,2,1,0:T(8,128)} %bitcast.3) | data formatting | bytes 1179648
  189.9 0.0 copy-done
  189.9 0.8 copy.11
Async XLA Ops:
  188.0 2.0 %copy-start = (f32[384,384]{1,0:T(8,128)S(1)}, f32[384,384]{1,0:T(8,128)}, u32[]{:S(2)}) copy-start(f32[384,384]{1,0:T(8,128)} %get-tuple-element.5) | copy-start | bytes 1769476
